TPU v7x, 32 devices: a whole 2x2x4 slice. The times are simulated.
32 devices in a mesh: arm: 2 (over y), snp: 16 (over z, x, core).
Axes of the slice: x: 2, y: 2, z: 4, core: 2. Of those that a mesh axis runs over, the one named last changes fastest.
Arguments:
- genotypes: int32 [4096, 1024], P(('arm', 'snp')), parts along dimension 0, may hold values from -2147483648 to 2147483647, as said below
- positions: int32 [4096], P(('arm', 'snp')), parts along dimension 0, may hold values from 2001303 to 5334144, as said below
Outputs:
- linkage: float32 [4096, 1664], P(('arm', 'snp')), parts along dimension 0
There are 2 independent parts, one for each index of `arm`. A program takes and returns all parts, laid end to end along the dimension named above; each array names one. Nothing has to cross between parts.
Inputs may be any that keep to these rules, and one draw needn't show every extreme that they name: `genotypes`: each word holds 16 two-bit codes: the call of sample s sits in bits 2 * (s // 1024) and 2 * (s // 1024) + 1 of word s mod 1024; codes 0, 1, 2 count alternate alleles and code 3 marks a missing call. `positions`: strictly increasing; consecutive SNPs lie 1303 or more base pairs apart.
All inputs are finite; a program needn't handle non-finite values.
Results may differ from a plain program's by a relative error of at most 0.0031.
Values may be sent and summed in bfloat16 or wider, within the bound.
A program may use at most 128 MiB of HBM per device.

v0:
```python
import functools

import jax
import jax.numpy as jnp
from jax import lax
from jax.experimental import pallas as pl
from jax.experimental.pallas import tpu as pltpu
from jax.sharding import PartitionSpec as P

REACH = 6
BAND_BP = 1000000
CODES = 16
GROUP = 4
SPLIT = 4096
MESH = pl.DeviceIdType.MESH


def kernel(
    devices, geno, pos, out, words, stats, scores, accs, parts, gathered, mirror, came,
    w0s, w0r, w1s, w1r, w2s, w2r, s0s, s0r, s1s, s1r, s2s, s2r, ps, pr, ms, mr,
):
    rows, width = geno.shape
    quarter = width // GROUP
    groups = devices // GROUP
    samples = CODES * width
    me = lax.axis_index("snp")
    g, q = me // GROUP, me % GROUP
    base = me - q
    mates = [q + 1 - 2 * lax.rem(q, 2), lax.rem(q + 2, GROUP), None]
    mates[2] = mates[1] + 1 - 2 * lax.rem(mates[1], 2)

    def remote(src, dst, ss, rs, target):
        return pltpu.make_async_remote_copy(
            src_ref=src, dst_ref=dst, send_sem=ss, recv_sem=rs,
            device_id={"snp": target}, device_id_type=MESH,
        )

    barrier = pltpu.get_barrier_semaphore()
    for mate in mates:
        pl.semaphore_signal(barrier, inc=1, device_id={"snp": base + mate}, device_id_type=MESH)
    for dg in (-2, -1, 1, 2):
        @pl.when((g + dg >= 0) & (g + dg < groups))
        def _():
            for m in range(GROUP):
                pl.semaphore_signal(
                    barrier, inc=1, device_id={"snp": base + dg * GROUP + m}, device_id_type=MESH
                )

    low = 0x55555555
    raw = geno[...]
    up = jnp.right_shift(raw, 1)
    miss = raw & up & low
    ones = raw & low & ~miss
    twos = up & low & ~miss

    def count(x):
        x = (x & 0x33333333) + (jnp.right_shift(x, 2) & 0x33333333)
        x = (x & 0x0F0F0F0F) + (jnp.right_shift(x, 4) & 0x0F0F0F0F)
        x = x + jnp.right_shift(x, 8)
        x = (x + jnp.right_shift(x, 16)) & 0x3F
        return jnp.sum(x.astype(jnp.float32), axis=1, keepdims=True)

    tally = samples - count(miss)
    allele = (count(ones) + 2.0 * count(twos) + 1.0) / (2.0 * tally + 2.0)
    spread = lax.rsqrt(2.0 * allele * (1.0 - allele))
    lane = lax.broadcasted_iota(jnp.int32, (rows, 128), 1)
    pair_t = jnp.where(lane < 2, 2.0 * allele, spread).T
    where_row = pos[...]
    hi = where_row // SPLIT
    lo = where_row - hi * SPLIT
    stats[0, q, 0:4, :] = pair_t[0:4, :]
    stats[0, q, 4:6, :] = jnp.broadcast_to(hi.astype(jnp.float32), (2, rows))
    stats[0, q, 6:8, :] = jnp.broadcast_to(lo.astype(jnp.float32), (2, rows))
    own_cols = pl.ds(pl.multiple_of(q * quarter, quarter), quarter)
    words[0, q] = geno[:, own_cols]
    out[...] = jnp.zeros_like(out)

    near = jnp.minimum(g, 2) + jnp.minimum(groups - 1 - g, 2)
    pl.semaphore_wait(barrier, 3 + GROUP * near)

    def word_copy(i):
        mate = mates[i]
        cols = pl.ds(pl.multiple_of(mate * quarter, quarter), quarter)
        return remote(geno.at[:, cols], words.at[0, q], w0s.at[i], w0r.at[q], base + mate)

    def down_one(m, src):
        return remote(src, words.at[1, m], w1s.at[m], w1r.at[m], me - GROUP)

    def down_two(m, src):
        return remote(src, words.at[2, m], w2s.at[m], w2r.at[m], me - 2 * GROUP)

    def stat_mate(i):
        return remote(stats.at[0, q], stats.at[0, q], s0s.at[i], s0r.at[q], base + mates[i])

    def stat_one(m):
        return remote(stats.at[0, q], stats.at[1, q], s1s.at[m], s1r.at[q], base - GROUP + m)

    def stat_two(m):
        return remote(stats.at[0, q], stats.at[2, q], s2s.at[m], s2r.at[q], base - 2 * GROUP + m)

    has_one, has_two = g >= 1, g >= 2
    up_one, up_two = g + 1 < groups, g + 2 < groups

    for i in range(3):
        word_copy(i).start()
    for i in range(3):
        stat_mate(i).start()

    @pl.when(has_one)
    def _():
        for m in range(GROUP):
            stat_one(m).start()
        down_one(q, geno.at[:, own_cols]).start()

    @pl.when(has_two & (q < 2))
    def _():
        for m in range(GROUP):
            stat_two(m).start()
        down_two(q, geno.at[:, own_cols]).start()

    def wait_recv(ref, sem):
        remote(ref, ref, sem, sem, me).wait_recv()

    def decode(dg, m, slot, row0):
        st = jnp.concatenate([stats[dg, m]] * (rows // 8), axis=0).T
        mean, dev = st[:, 0:1], st[:, 2:3]
        packed = words[dg, m]

        def step(k, _):
            code = jnp.right_shift(packed, 2 * k) & 3
            z = (code.astype(jnp.float32) - mean) * dev
            z = jnp.where(code == 3, 0.0, z).astype(jnp.bfloat16)
            scores[slot, pl.ds(pl.multiple_of(row0, rows), rows),
                   pl.ds(pl.multiple_of(k * quarter, quarter), quarter)] = z
            return 0

        lax.fori_loop(0, CODES, step, 0, unroll=2)

    decode(0, q, q // 2, (q % 2) * rows)
    for mate in mates:
        wait_recv(words.at[0, mate], w0r.at[mate])

        @pl.when(has_one)
        def _():
            down_one(mate, words.at[0, mate]).start()

        @pl.when(has_two & (mate < 2))
        def _():
            down_two(mate, words.at[0, mate]).start()

        wait_recv(stats.at[0, mate], s0r.at[mate])
        decode(0, mate, mate // 2, (mate % 2) * rows)

    def part_copy(t, i):
        return remote(parts.at[t, mates[i]], gathered.at[t, q], ps.at[t, i], pr.at[t, q], base + mates[i])

    def product(t, slot, first):
        right = scores[slot]
        for half in range(first, 2):
            block = lax.dot_general(
                scores[half], right, (((1,), (1,)), ((), ())), preferred_element_type=jnp.float32
            )
            accs[t, 2 * half] = block[:rows]
            accs[t, 2 * half + 1] = block[rows:]
            parts[t, 2 * half] = block[:rows].astype(jnp.bfloat16)
            parts[t, 2 * half + 1] = block[rows:].astype(jnp.bfloat16)

    first_pair = q // 2
    steps = [(0, first_pair), (0, 1 - first_pair), (1, first_pair), (1, 1 - first_pair), (2, 0)]
    slots = [first_pair, 1 - first_pair, 2 + first_pair, 3 - first_pair, 4]

    own_pos = jnp.concatenate([stats[0, q]] * (rows // 8), axis=0).T
    own_at = own_pos[:, 4:5].astype(jnp.int32) * SPLIT + own_pos[:, 6:7].astype(jnp.int32)

    def mirror_copy(t, m2, offset):
        return remote(
            mirror.at[t, m2], came.at[offset - 1], ms.at[t, m2], mr.at[offset - 1], me + offset
        )

    def finish(n):
        dg, pair = steps[n]
        t = slots[n]
        total = accs[t, q]
        for mate in mates:
            wait_recv(gathered.at[t, mate], pr.at[t, mate])
            total = total + gathered[t, mate].astype(jnp.float32)
        total = total / samples
        for m2 in range(2):
            m = 2 * pair + m2
            offset = dg * GROUP + m - q
            st = stats[dg, m]
            their = st[4:5, :].astype(jnp.int32) * SPLIT + st[6:7, :].astype(jnp.int32)
            block = total[:, m2 * rows:(m2 + 1) * rows]
            block = jnp.where(jnp.abs(own_at - their) <= BAND_BP, block, 0.0)
            cols = pl.ds(pl.multiple_of((REACH + offset) * rows, rows), rows)
            if dg == 0:
                out[:, cols] = block
            else:
                @pl.when(offset <= REACH)
                def _():
                    out[:, cols] = block
                    mirror[t, m2] = block.astype(jnp.bfloat16)
                    mirror_copy(t, m2, offset).start()

    def run(n):
        dg, pair = steps[n]
        if dg == 0:
            slot = pair
        else:
            slot = n
            for m2 in range(2):
                m = 2 * pair + m2
                wait_recv(words.at[dg, m], (w1r if dg == 1 else w2r).at[m])
                wait_recv(stats.at[dg, m], (s1r if dg == 1 else s2r).at[m])
                decode(dg, m, slot, m2 * rows)
        product(slots[n], slot, 1 if dg == 2 else 0)
        for i in range(3):
            if dg == 2:
                @pl.when(mates[i] >= 2)
                def _():
                    part_copy(slots[n], i).start()
            else:
                part_copy(slots[n], i).start()

    run(0)
    run(1)

    @pl.when(up_one)
    def _():
        run(2)
        finish(0)
        finish(1)
        run(3)
        finish(2)

    @pl.when(jnp.logical_not(up_one))
    def _():
        finish(0)
        finish(1)

    @pl.when(up_two)
    def _():
        run(4)

    @pl.when(up_one)
    def _():
        finish(3)

    @pl.when(up_two & (q >= 2))
    def _():
        finish(4)

    for offset in range(1, REACH + 1):
        @pl.when((offset > q) & (me >= offset))
        def _():
            wait_recv(came.at[offset - 1], mr.at[offset - 1])
            out[:, (REACH - offset) * rows:(REACH - offset + 1) * rows] = (
                came[offset - 1].astype(jnp.float32).T
            )

    for i in range(3):
        word_copy(i).wait_send()
        stat_mate(i).wait_send()
        part_copy(slots[0], i).wait_send()
        part_copy(slots[1], i).wait_send()

    @pl.when(has_one)
    def _():
        for m in range(GROUP):
            stat_one(m).wait_send()
            down_one(m, words.at[0, m]).wait_send()

    @pl.when(has_two)
    def _():
        for m in range(2):
            down_two(m, words.at[0, m]).wait_send()

    @pl.when(has_two & (q < 2))
    def _():
        for m in range(GROUP):
            stat_two(m).wait_send()

    @pl.when(up_one)
    def _():
        for n in (2, 3):
            for i in range(3):
                part_copy(slots[n], i).wait_send()

    @pl.when(up_two)
    def _():
        for i in range(3):
            @pl.when(mates[i] >= 2)
            def _():
                part_copy(slots[4], i).wait_send()

    for n, there in ((2, up_one), (3, up_one), (4, up_two & (q >= 2))):
        dg, pair = steps[n]
        for m2 in range(2):
            offset = dg * GROUP + 2 * pair + m2 - q

            @pl.when(there & (offset <= REACH))
            def _():
                mirror_copy(slots[n], m2, offset).wait_send()


def per_device(devices, genotypes, positions):
    rows, width = genotypes.shape
    quarter = width // GROUP
    dma = pltpu.SemaphoreType.DMA
    vmem = pl.BlockSpec(memory_space=pltpu.VMEM)
    return pl.pallas_call(
        functools.partial(kernel, devices),
        out_shape=jax.ShapeDtypeStruct((rows, (2 * REACH + 1) * rows), jnp.float32),
        in_specs=[vmem, vmem],
        out_specs=vmem,
        scratch_shapes=[
            pltpu.VMEM((3, GROUP, rows, quarter), jnp.int32),
            pltpu.VMEM((3, GROUP, 8, rows), jnp.float32),
            pltpu.VMEM((5, 2 * rows, CODES * quarter), jnp.bfloat16),
            pltpu.VMEM((5, GROUP, rows, 2 * rows), jnp.float32),
            pltpu.VMEM((5, GROUP, rows, 2 * rows), jnp.bfloat16),
            pltpu.VMEM((5, GROUP, rows, 2 * rows), jnp.bfloat16),
            pltpu.VMEM((5, 2, rows, rows), jnp.bfloat16),
            pltpu.VMEM((REACH, rows, rows), jnp.bfloat16),
            dma((3,)), dma((GROUP,)),
            dma((GROUP,)), dma((GROUP,)),
            dma((GROUP,)), dma((GROUP,)),
            dma((3,)), dma((GROUP,)),
            dma((GROUP,)), dma((GROUP,)),
            dma((GROUP,)), dma((GROUP,)),
            dma((5, 3)), dma((5, GROUP)),
            dma((5, 2)), dma((REACH,)),
        ],
        compiler_params=pltpu.CompilerParams(
            collective_id=0, has_side_effects=True, vmem_limit_bytes=60000000
        ),
    )(genotypes, positions[None, :])


def solution(mesh):
    return jax.shard_map(
        functools.partial(per_device, mesh.shape["snp"]),
        mesh=mesh,
        in_specs=(P(("arm", "snp"), None), P(("arm", "snp"))),
        out_specs=P(("arm", "snp"), None),
        check_vma=False,
    )
```

profile of v0, /device:TPU:25, one launch (start us, length us, event | category | flops | bytes accessed | tf_op | source)
XLA Modules:
  0.0 50.4 jit_solution(8868850714376914262)
XLA Ops:
  0.0 48.3 %shard_map.28 = f32[128,1664]{1,0:T(8,128)} custom-call(s32[128,1024]{1,0:T(8,128)} %geno.1, s32[1,128]{1,0:T(1,128)} %bitcast.1), custom_call_target="tpu_custom_call" | custom-call | tf_op jit(solution)/shard_map/pallas_call | solution.py:311
  48.3 2.1 %copy.4 = f32[128,1664]{1,0:T(8,128)} copy(f32[128,1664]{1,0:T(8,128)} %shard_map.28) | data formatting | bytes 1703936
where the time goes:
time: 50.5 us; the launch traced here: 50.4 us
  Pallas kernels  48.3 us (96%)
  local copies, waits for them, and re-layouts  2.11 us (4%)
    pallas_call x1, Pallas kernels, per_device(): pl.pallas_call(functools.partial(kernel, devices), out_shape=jax.ShapeDty...  48.3 us
    unnamed x1, local copies, waits for them, and re-layouts  2.11 us

commit v1 on v0

--- a/solution.py
+++ b/solution.py
@@ -16,7 +16,7 @@
 
 
 def kernel(
-    devices, geno, pos, out, words, stats, scores, accs, parts, gathered, mirror, came,
+    devices, geno, pos, out, words, stats, scores, accs, parts, gathered, sums, mirror, came, spans,
     w0s, w0r, w1s, w1r, w2s, w2r, s0s, s0r, s1s, s1r, s2s, s2r, ps, pr, ms, mr,
 ):
     rows, width = geno.shape
@@ -86,8 +86,8 @@
     def down_one(m, src):
         return remote(src, words.at[1, m], w1s.at[m], w1r.at[m], me - GROUP)
 
-    def down_two(m, src):
-        return remote(src, words.at[2, m], w2s.at[m], w2r.at[m], me - 2 * GROUP)
+    def up_words(m, src):
+        return remote(src, words.at[2, m - 2], w2s.at[m - 2], w2r.at[m - 2], me + 2 * GROUP)
 
     def stat_mate(i):
         return remote(stats.at[0, q], stats.at[0, q], s0s.at[i], s0r.at[q], base + mates[i])
@@ -96,7 +96,7 @@
         return remote(stats.at[0, q], stats.at[1, q], s1s.at[m], s1r.at[q], base - GROUP + m)
 
     def stat_two(m):
-        return remote(stats.at[0, q], stats.at[2, q], s2s.at[m], s2r.at[q], base - 2 * GROUP + m)
+        return remote(stats.at[0, q], stats.at[2, q - 2], s2s.at[m], s2r.at[q - 2], base + 2 * GROUP + m)
 
     has_one, has_two = g >= 1, g >= 2
     up_one, up_two = g + 1 < groups, g + 2 < groups
@@ -112,29 +112,35 @@
             stat_one(m).start()
         down_one(q, geno.at[:, own_cols]).start()
 
-    @pl.when(has_two & (q < 2))
+    @pl.when(up_two & (q >= 2))
     def _():
         for m in range(GROUP):
             stat_two(m).start()
-        down_two(q, geno.at[:, own_cols]).start()
+        up_words(q, geno.at[:, own_cols]).start()
 
     def wait_recv(ref, sem):
         remote(ref, ref, sem, sem, me).wait_recv()
 
     def decode(dg, m, slot, row0):
         st = jnp.concatenate([stats[dg, m]] * (rows // 8), axis=0).T
-        mean, dev = st[:, 0:1], st[:, 2:3]
-        packed = words[dg, m]
-
-        def step(k, _):
-            code = jnp.right_shift(packed, 2 * k) & 3
-            z = (code.astype(jnp.float32) - mean) * dev
-            z = jnp.where(code == 3, 0.0, z).astype(jnp.bfloat16)
-            scores[slot, pl.ds(pl.multiple_of(row0, rows), rows),
-                   pl.ds(pl.multiple_of(k * quarter, quarter), quarter)] = z
+        spans[0] = jnp.broadcast_to(st[:, 0:1], (rows, 128))
+        spans[1] = jnp.broadcast_to(st[:, 2:3], (rows, 128))
+
+        def step(r, _):
+            some = pl.ds(pl.multiple_of(r * 16, 16), 16)
+            there = pl.ds(pl.multiple_of(row0 + r * 16, 16), 16)
+            mean, dev = spans[0, some, :], spans[1, some, :]
+            for part in range(quarter // 128):
+                packed = words[dg, m, some, part * 128:(part + 1) * 128]
+                for k in range(CODES):
+                    code = jnp.right_shift(packed, 2 * k) & 3
+                    z = (code.astype(jnp.float32) - mean) * dev
+                    z = jnp.where(code == 3, 0.0, z).astype(jnp.bfloat16)
+                    at = k * quarter + part * 128
+                    scores[slot, there, at:at + 128] = z
             return 0
 
-        lax.fori_loop(0, CODES, step, 0, unroll=2)
+        lax.fori_loop(0, rows // 16, step, 0, unroll=2)
 
     decode(0, q, q // 2, (q % 2) * rows)
     for mate in mates:
@@ -144,19 +150,34 @@
         def _():
             down_one(mate, words.at[0, mate]).start()
 
-        @pl.when(has_two & (mate < 2))
+        @pl.when(up_two & (mate >= 2))
         def _():
-            down_two(mate, words.at[0, mate]).start()
+            up_words(mate, words.at[0, mate]).start()
 
         wait_recv(stats.at[0, mate], s0r.at[mate])
         decode(0, mate, mate // 2, (mate % 2) * rows)
 
-    def part_copy(t, i):
-        return remote(parts.at[t, mates[i]], gathered.at[t, q], ps.at[t, i], pr.at[t, q], base + mates[i])
-
-    def product(t, slot, first):
+    twin, across = mates[0], mates[1]
+    twin_across = lax.rem(twin + 2, GROUP)
+
+    def to_twin(t):
+        return remote(parts.at[t, twin], gathered.at[t, 0], ps.at[t, 0], pr.at[t, 0], base + twin)
+
+    def via_twin(t):
+        return remote(parts.at[t, twin_across], gathered.at[t, 1], ps.at[t, 1], pr.at[t, 1], base + twin)
+
+    def to_across(t):
+        return remote(sums.at[t], gathered.at[t, 2], ps.at[t, 2], pr.at[t, 2], base + across)
+
+    def forward(n):
+        t = slots[n]
+        wait_recv(gathered.at[t, 1], pr.at[t, 1])
+        sums[t] = (accs[t, across] + gathered[t, 1].astype(jnp.float32)).astype(jnp.bfloat16)
+        to_across(t).start()
+
+    def product(t, slot, halves):
         right = scores[slot]
-        for half in range(first, 2):
+        for half in range(halves):
             block = lax.dot_general(
                 scores[half], right, (((1,), (1,)), ((), ())), preferred_element_type=jnp.float32
             )
@@ -172,22 +193,25 @@
     own_pos = jnp.concatenate([stats[0, q]] * (rows // 8), axis=0).T
     own_at = own_pos[:, 4:5].astype(jnp.int32) * SPLIT + own_pos[:, 6:7].astype(jnp.int32)
 
+    def reach_of(n, m2):
+        dg, pair = steps[n]
+        return (m2 + 2 - 2 * GROUP if dg == 2 else dg * GROUP + 2 * pair + m2) - q
+
     def mirror_copy(t, m2, offset):
-        return remote(
-            mirror.at[t, m2], came.at[offset - 1], ms.at[t, m2], mr.at[offset - 1], me + offset
-        )
+        slot = jnp.where(offset > 0, offset - 1, REACH - 1 - offset)
+        return remote(mirror.at[t, m2], came.at[slot], ms.at[t, m2], mr.at[slot], me + offset)
 
     def finish(n):
         dg, pair = steps[n]
         t = slots[n]
         total = accs[t, q]
-        for mate in mates:
-            wait_recv(gathered.at[t, mate], pr.at[t, mate])
-            total = total + gathered[t, mate].astype(jnp.float32)
+        for source in (0, 2):
+            wait_recv(gathered.at[t, source], pr.at[t, source])
+            total = total + gathered[t, source].astype(jnp.float32)
         total = total / samples
         for m2 in range(2):
             m = 2 * pair + m2
-            offset = dg * GROUP + m - q
+            offset = reach_of(n, m2)
             st = stats[dg, m]
             their = st[4:5, :].astype(jnp.int32) * SPLIT + st[6:7, :].astype(jnp.int32)
             block = total[:, m2 * rows:(m2 + 1) * rows]
@@ -196,7 +220,7 @@
             if dg == 0:
                 out[:, cols] = block
             else:
-                @pl.when(offset <= REACH)
+                @pl.when((offset <= REACH) & (offset >= -REACH))
                 def _():
                     out[:, cols] = block
                     mirror[t, m2] = block.astype(jnp.bfloat16)
@@ -213,56 +237,72 @@
                 wait_recv(words.at[dg, m], (w1r if dg == 1 else w2r).at[m])
                 wait_recv(stats.at[dg, m], (s1r if dg == 1 else s2r).at[m])
                 decode(dg, m, slot, m2 * rows)
-        product(slots[n], slot, 1 if dg == 2 else 0)
-        for i in range(3):
-            if dg == 2:
-                @pl.when(mates[i] >= 2)
-                def _():
-                    part_copy(slots[n], i).start()
-            else:
-                part_copy(slots[n], i).start()
+        product(slots[n], slot, 1 if dg == 2 else 2)
+        if dg == 2:
+            @pl.when(q < 2)
+            def _():
+                to_twin(slots[n]).start()
+
+            @pl.when(q >= 2)
+            def _():
+                via_twin(slots[n]).start()
+        else:
+            via_twin(slots[n]).start()
+            to_twin(slots[n]).start()
 
     run(0)
     run(1)
+    forward(0)
+
+    @pl.when(has_two)
+    def _():
+        run(4)
+
+    forward(1)
 
     @pl.when(up_one)
     def _():
         run(2)
-        finish(0)
-        finish(1)
+
+    @pl.when(has_two & (q >= 2))
+    def _():
+        forward(4)
+
+    finish(0)
+    finish(1)
+
+    @pl.when(up_one)
+    def _():
+        forward(2)
         run(3)
+        forward(3)
+
+    @pl.when(has_two & (q < 2))
+    def _():
+        finish(4)
+
+    @pl.when(up_one)
+    def _():
         finish(2)
-
-    @pl.when(jnp.logical_not(up_one))
-    def _():
-        finish(0)
-        finish(1)
-
-    @pl.when(up_two)
-    def _():
-        run(4)
-
-    @pl.when(up_one)
-    def _():
         finish(3)
 
-    @pl.when(up_two & (q >= 2))
-    def _():
-        finish(4)
+    def take(slot, col):
+        wait_recv(came.at[slot], mr.at[slot])
+        out[:, col * rows:(col + 1) * rows] = came[slot].astype(jnp.float32).T
 
     for offset in range(1, REACH + 1):
-        @pl.when((offset > q) & (me >= offset))
+        if offset > GROUP:
+            @pl.when((offset + q >= 2 * GROUP) & up_two)
+            def _():
+                take(REACH + offset - 1, REACH + offset)
+
+        @pl.when((offset > q) & (offset <= q + GROUP) & has_one)
         def _():
-            wait_recv(came.at[offset - 1], mr.at[offset - 1])
-            out[:, (REACH - offset) * rows:(REACH - offset + 1) * rows] = (
-                came[offset - 1].astype(jnp.float32).T
-            )
+            take(offset - 1, REACH - offset)
 
     for i in range(3):
         word_copy(i).wait_send()
         stat_mate(i).wait_send()
-        part_copy(slots[0], i).wait_send()
-        part_copy(slots[1], i).wait_send()
 
     @pl.when(has_one)
     def _():
@@ -270,35 +310,42 @@
             stat_one(m).wait_send()
             down_one(m, words.at[0, m]).wait_send()
 
-    @pl.when(has_two)
-    def _():
-        for m in range(2):
-            down_two(m, words.at[0, m]).wait_send()
-
-    @pl.when(has_two & (q < 2))
+    @pl.when(up_two)
+    def _():
+        for m in (2, 3):
+            up_words(m, words.at[0, m]).wait_send()
+
+    @pl.when(up_two & (q >= 2))
     def _():
         for m in range(GROUP):
             stat_two(m).wait_send()
 
+    def left(n):
+        for copy in (to_twin, via_twin, to_across):
+            copy(slots[n]).wait_send()
+
+    left(0)
+    left(1)
+
     @pl.when(up_one)
     def _():
-        for n in (2, 3):
-            for i in range(3):
-                part_copy(slots[n], i).wait_send()
-
-    @pl.when(up_two)
-    def _():
-        for i in range(3):
-            @pl.when(mates[i] >= 2)
-            def _():
-                part_copy(slots[4], i).wait_send()
-
-    for n, there in ((2, up_one), (3, up_one), (4, up_two & (q >= 2))):
-        dg, pair = steps[n]
+        left(2)
+        left(3)
+
+    @pl.when(has_two & (q < 2))
+    def _():
+        to_twin(4).wait_send()
+
+    @pl.when(has_two & (q >= 2))
+    def _():
+        via_twin(4).wait_send()
+        to_across(4).wait_send()
+
+    for n, there in ((2, up_one), (3, up_one), (4, has_two & (q < 2))):
         for m2 in range(2):
-            offset = dg * GROUP + 2 * pair + m2 - q
-
-            @pl.when(there & (offset <= REACH))
+            offset = reach_of(n, m2)
+
+            @pl.when(there & (offset <= REACH) & (offset >= -REACH))
             def _():
                 mirror_copy(slots[n], m2, offset).wait_send()
 
@@ -319,17 +366,19 @@
             pltpu.VMEM((5, 2 * rows, CODES * quarter), jnp.bfloat16),
             pltpu.VMEM((5, GROUP, rows, 2 * rows), jnp.float32),
             pltpu.VMEM((5, GROUP, rows, 2 * rows), jnp.bfloat16),
-            pltpu.VMEM((5, GROUP, rows, 2 * rows), jnp.bfloat16),
+            pltpu.VMEM((5, 3, rows, 2 * rows), jnp.bfloat16),
+            pltpu.VMEM((5, rows, 2 * rows), jnp.bfloat16),
             pltpu.VMEM((5, 2, rows, rows), jnp.bfloat16),
-            pltpu.VMEM((REACH, rows, rows), jnp.bfloat16),
+            pltpu.VMEM((2 * REACH, rows, rows), jnp.bfloat16),
+            pltpu.VMEM((2, rows, 128), jnp.float32),
             dma((3,)), dma((GROUP,)),
             dma((GROUP,)), dma((GROUP,)),
             dma((GROUP,)), dma((GROUP,)),
             dma((3,)), dma((GROUP,)),
             dma((GROUP,)), dma((GROUP,)),
             dma((GROUP,)), dma((GROUP,)),
-            dma((5, 3)), dma((5, GROUP)),
-            dma((5, 2)), dma((REACH,)),
+            dma((5, 3)), dma((5, 3)),
+            dma((5, 2)), dma((2 * REACH,)),
         ],
         compiler_params=pltpu.CompilerParams(
             collective_id=0, has_side_effects=True, vmem_limit_bytes=60000000

time: 50.5 us -> 39 us (0.77)
  the two profiles are of different devices: /device:TPU:25 before, /device:TPU:17 now
where the time goes in v1:
time: 39 us; the launch traced here: 38.8 us
  Pallas kernels  36.7 us (94%)
  local copies, waits for them, and re-layouts  2.11 us (5%)
    pallas_call x1, Pallas kernels, per_device(): pl.pallas_call(functools.partial(kernel, devices), out_shape=jax.ShapeDty...  36.7 us
    unnamed x1, local copies, waits for them, and re-layouts  2.11 us

profile of v1, /device:TPU:17, one launch (start us, length us, event | category | flops | bytes accessed | tf_op | source)
XLA Modules:
  0.0 38.8 jit_solution(7127729502267010027)
XLA Ops:
  0.0 36.7 %shard_map.28 = f32[128,1664]{1,0:T(8,128)} custom-call(s32[128,1024]{1,0:T(8,128)} %geno.1, s32[1,128]{1,0:T(1,128)} %bitcast.1), custom_call_target="tpu_custom_call" | custom-call | tf_op jit(solution)/shard_map/pallas_call | solution.py:358
  36.7 2.1 %copy.4 = f32[128,1664]{1,0:T(8,128)} copy(f32[128,1664]{1,0:T(8,128)} %shard_map.28) | data formatting | bytes 1703936

commit v2 on v1

--- a/solution.py
+++ b/solution.py
@@ -102,21 +102,20 @@
     up_one, up_two = g + 1 < groups, g + 2 < groups
 
     for i in range(3):
+        stat_mate(i).start()
         word_copy(i).start()
-    for i in range(3):
-        stat_mate(i).start()
 
     @pl.when(has_one)
     def _():
+        down_one(q, geno.at[:, own_cols]).start()
         for m in range(GROUP):
             stat_one(m).start()
-        down_one(q, geno.at[:, own_cols]).start()
 
     @pl.when(up_two & (q >= 2))
     def _():
+        up_words(q, geno.at[:, own_cols]).start()
         for m in range(GROUP):
             stat_two(m).start()
-        up_words(q, geno.at[:, own_cols]).start()
 
     def wait_recv(ref, sem):
         remote(ref, ref, sem, sem, me).wait_recv()
@@ -226,18 +225,17 @@
                     mirror[t, m2] = block.astype(jnp.bfloat16)
                     mirror_copy(t, m2, offset).start()
 
-    def run(n):
+    def ready(n):
         dg, pair = steps[n]
-        if dg == 0:
-            slot = pair
-        else:
-            slot = n
-            for m2 in range(2):
-                m = 2 * pair + m2
-                wait_recv(words.at[dg, m], (w1r if dg == 1 else w2r).at[m])
-                wait_recv(stats.at[dg, m], (s1r if dg == 1 else s2r).at[m])
-                decode(dg, m, slot, m2 * rows)
-        product(slots[n], slot, 1 if dg == 2 else 2)
+        for m2 in range(2):
+            m = 2 * pair + m2
+            wait_recv(words.at[dg, m], (w1r if dg == 1 else w2r).at[m])
+            wait_recv(stats.at[dg, m], (s1r if dg == 1 else s2r).at[m])
+            decode(dg, m, n, m2 * rows)
+
+    def combine(n):
+        dg, pair = steps[n]
+        product(slots[n], pair if dg == 0 else n, 1 if dg == 2 else 2)
         if dg == 2:
             @pl.when(q < 2)
             def _():
@@ -250,41 +248,49 @@
             via_twin(slots[n]).start()
             to_twin(slots[n]).start()
 
-    run(0)
-    run(1)
+    combine(0)
+
+    @pl.when(has_two)
+    def _():
+        ready(4)
+        combine(4)
+
     forward(0)
 
-    @pl.when(has_two)
-    def _():
-        run(4)
+    @pl.when(up_one)
+    def _():
+        ready(2)
+        combine(2)
+
+    @pl.when(has_two & (q >= 2))
+    def _():
+        forward(4)
+
+    @pl.when(up_one)
+    def _():
+        ready(3)
+        forward(2)
+        combine(3)
+
+    @pl.when(has_two & (q < 2))
+    def _():
+        finish(4)
+
+    combine(1)
+
+    @pl.when(up_one)
+    def _():
+        forward(3)
 
     forward(1)
 
     @pl.when(up_one)
     def _():
-        run(2)
-
-    @pl.when(has_two & (q >= 2))
-    def _():
-        forward(4)
+        finish(2)
+        finish(3)
 
     finish(0)
     finish(1)
-
-    @pl.when(up_one)
-    def _():
-        forward(2)
-        run(3)
-        forward(3)
-
-    @pl.when(has_two & (q < 2))
-    def _():
-        finish(4)
-
-    @pl.when(up_one)
-    def _():
-        finish(2)
-        finish(3)
 
     def take(slot, col):
         wait_recv(came.at[slot], mr.at[slot])

time: 39 us -> 39.1 us (level)
  the two profiles are of different devices: /device:TPU:17 before, /device:TPU:25 now
where the time goes in v2:
time: 39.1 us; the launch traced here: 39 us
  Pallas kernels  36.9 us (94%)
  local copies, waits for them, and re-layouts  2.11 us (5%)
    pallas_call x1, Pallas kernels, per_device(): pl.pallas_call(functools.partial(kernel, devices), out_shape=jax.ShapeDty...  36.9 us
    unnamed x1, local copies, waits for them, and re-layouts  2.11 us

profile of v2, /device:TPU:25, one launch (start us, length us, event | category | flops | bytes accessed | tf_op | source)
XLA Modules:
  0.0 39.0 jit_solution(18335739486894331996)
XLA Ops:
  0.0 36.9 %shard_map.28 = f32[128,1664]{1,0:T(8,128)} custom-call(s32[128,1024]{1,0:T(8,128)} %geno.1, s32[1,128]{1,0:T(1,128)} %bitcast.1), custom_call_target="tpu_custom_call" | custom-call | tf_op jit(solution)/shard_map/pallas_call | solution.py:364
  36.9 2.1 %copy.4 = f32[128,1664]{1,0:T(8,128)} copy(f32[128,1664]{1,0:T(8,128)} %shard_map.28) | data formatting | bytes 1703936

commit v3 on v2

--- a/solution.py
+++ b/solution.py
@@ -185,7 +185,7 @@
             parts[t, 2 * half] = block[:rows].astype(jnp.bfloat16)
             parts[t, 2 * half + 1] = block[rows:].astype(jnp.bfloat16)
 
-    first_pair = q // 2
+    first_pair = 0
     steps = [(0, first_pair), (0, 1 - first_pair), (1, first_pair), (1, 1 - first_pair), (2, 0)]
     slots = [first_pair, 1 - first_pair, 2 + first_pair, 3 - first_pair, 4]
 
@@ -282,11 +282,14 @@
     def _():
         forward(3)
 
+    @pl.when(up_one)
+    def _():
+        finish(2)
+
     forward(1)
 
     @pl.when(up_one)
     def _():
-        finish(2)
         finish(3)
 
     finish(0)

time: 39.1 us -> 35.9 us (0.918)
  the two profiles are of different devices: /device:TPU:25 before, /device:TPU:31 now
where the time goes in v3:
time: 35.9 us; the launch traced here: 35.7 us
  Pallas kernels  33.6 us (94%)
  local copies, waits for them, and re-layouts  2.11 us (6%)
    pallas_call x1, Pallas kernels, per_device(): pl.pallas_call(functools.partial(kernel, devices), out_shape=jax.ShapeDty...  33.6 us
    unnamed x1, local copies, waits for them, and re-layouts  2.11 us

profile of v3, /device:TPU:31, one launch (start us, length us, event | category | flops | bytes accessed | tf_op | source)
XLA Modules:
  0.0 35.7 jit_solution(2398769003153303310)
XLA Ops:
  0.0 33.6 %shard_map.28 = f32[128,1664]{1,0:T(8,128)} custom-call(s32[128,1024]{1,0:T(8,128)} %geno.1, s32[1,128]{1,0:T(1,128)} %bitcast.1), custom_call_target="tpu_custom_call" | custom-call | tf_op jit(solution)/shard_map/pallas_call | solution.py:367
  33.6 2.1 %copy.4 = f32[128,1664]{1,0:T(8,128)} copy(f32[128,1664]{1,0:T(8,128)} %shard_map.28) | data formatting | bytes 1703936
